TPU v7x, 32 devices: a whole 2x2x4 slice. The times are simulated.
32 devices in a mesh: row: 8 (over z, x), col: 4 (over y, core).
Axes of the slice: x: 2, y: 2, z: 4, core: 2. Of those that a mesh axis runs over, the one named last changes fastest.
Arguments:
- basis_blocks: float32 [8, 16, 262144], P(None, None, ('col', 'row')), may hold values from -6 to 6
- tile_values: bfloat16 [4, 8, 384, 128, 128], P('col', 'row'), may hold values from -0.375 to 0.375
- tile_rows: int32 [4, 8, 384], P('col', 'row'), may hold values from 0 to 511
- tile_column: int32 [4, 8, 384], P('col', 'row'), may hold values from 0 to 255
- tile_count: int32 [4, 8], P('col', 'row'), may hold values from 1 to 384, as said below
- diagonal: float32 [262144], P(('col', 'row')), may hold values from 1 to 6
Outputs:
- new_block: float32 [16, 262144], P(None, ('col', 'row'))
- coefficients: float32 [8, 16, 16], replicated
- triangle: float32 [16, 16], replicated
Inputs may be any that keep to these rules, and one draw needn't show every extreme that they name: Each operator block stores tile_count tiles in its first slots; at most 384, and some block has exactly 384 in every draw. Slots past the count hold arbitrary data and are ignored.
All inputs are finite; a program needn't handle non-finite values.
Results may differ from a plain program's by a relative error of at most 0.0031.
Values may be sent and summed in bfloat16 or wider, within the bound.
A program may use at most 128 MiB of HBM per device.

v0:
```python
import jax
import jax.numpy as jnp
from jax import lax
from jax.sharding import PartitionSpec as P


def local(basis_blocks, tile_values, tile_rows, tile_column, tile_count, diagonal):
    rhs_width = basis_blocks.shape[1]
    seg_rows = basis_blocks.shape[2]
    total_rows = seg_rows * lax.axis_size("row") * lax.axis_size("col")
    block_tiles = lax.axis_size("row") * seg_rows // 128
    vector = basis_blocks[-1].astype(jnp.bfloat16)
    expanded = lax.all_gather(vector, "col", axis=1, tiled=True)
    xblocks = expanded.reshape(rhs_width, -1, 128)
    values = tile_values[0, 0]
    row_ids = tile_rows[0, 0]
    column_ids = tile_column[0, 0]
    live_count = tile_count[0, 0]
    live_tiles = jnp.arange(values.shape[0], dtype=jnp.int32) < live_count
    gathered = jnp.take(xblocks, column_ids, axis=1)
    products = jnp.einsum("stj,tji->tsi", gathered, values, preferred_element_type=jnp.float32)
    inside = live_tiles & (row_ids >= 0) & (row_ids < 0 + block_tiles)
    segment_ids = jnp.where(inside, row_ids - 0, block_tiles)
    summed = jax.ops.segment_sum(products, segment_ids, num_segments=block_tiles + 1)
    folded = lax.psum_scatter(summed[:block_tiles], "row", scatter_dimension=0, tiled=True)
    image_rows = folded.transpose(1, 0, 2).reshape(rhs_width, seg_rows)
    image_rows = image_rows + diagonal[None, :] * basis_blocks[-1]
    highest = lax.Precision.HIGHEST
    local_proj = jnp.einsum("kap,bp->kab", basis_blocks, image_rows, precision=highest)
    local_self = jnp.dot(image_rows, image_rows.T, precision=highest)
    local_basis = jnp.einsum("kap,lcp->kalc", basis_blocks, basis_blocks, precision=highest)
    proj_sum, image_sum, basis_sum = lax.psum((local_proj, local_self, local_basis), ("row", "col"))
    coefficients = proj_sum / total_rows
    image_gram = image_sum / total_rows
    basis_gram = basis_sum / total_rows
    projected = image_rows - jnp.einsum(
        "kab,kap->bp", coefficients, basis_blocks, precision=highest
    )
    cross_term = jnp.einsum("kab,kad->bd", coefficients, coefficients, precision=highest)
    basis_term = jnp.einsum(
        "kab,kalc,lcd->bd", coefficients, basis_gram, coefficients, precision=highest
    )
    gram_matrix = image_gram - 2.0 * cross_term + basis_term
    lower_factor = jnp.linalg.cholesky(gram_matrix)
    new_block = lax.linalg.triangular_solve(lower_factor, projected, left_side=True, lower=True)
    return (new_block, coefficients, lower_factor.T)


def solution(mesh):
    in_specs = (
        P(None, None, ("col", "row")),
        P("col", "row", None, None, None),
        P("col", "row", None),
        P("col", "row", None),
        P("col", "row"),
        P(("col", "row")),
    )
    out_specs = (P(None, ("col", "row")), P(), P())
    return jax.shard_map(local, mesh=mesh, in_specs=in_specs, out_specs=out_specs, check_vma=False)
```

profile of v0, /device:TPU:0, one launch (start us, length us, event | category | flops | bytes accessed | tf_op | source)
XLA Modules:
  0.0 285.5 jit_solution(4340497072909810050)
XLA Ops:
  8.0 0.0 all-gather.2.cloned.1.call-start
  8.0 1.8 bitcast_convert_fusion
  9.8 0.0 all-gather.2.cloned.1.call-update
  9.8 0.0 reduce-scatter.2.cloned.1.call-start
  10.5 0.7 reduce.7
  11.2 0.7 fusion.22
  11.9 0.7 fusion.23
  12.7 17.7 %all-gather.2.cloned.1.call-done = bf16[16,32768]{1,0:T(8,128)(2,1)} async-done(((bf16[16,8192]{1,0:T(8,128)(2,1)}), bf16[16,32768]{1,0:T(8,128)(2,1)}) %all-gather.2.cloned.1.call-update) | async-done | bytes 1048592 | tf_op jit(solution)/shard_map/all_gather | solution.py:13
  30.4 1.4 copy_bitcast_fusion
  31.8 2.6 gather_fusion
  34.4 6.9 %fusion = f32[384,16,128]{2,1,0:T(8,128)S(1)} fusion(bf16[1,1,384,128,128]{4,3,2,1,0:T(8,128)(2,1)} %param.7, bf16[384,16,128]{2,1,0:T(8,128)(2,1)} %gather_fusion, pred[384]{0:T(512)(128)(4,1)S(1)} %compare_and_fusion), kind=kOutput, calls=%fused_computation.2 | convolution fusion | flops 202113024 | bytes 17301888 | tf_op jit(solution)/shard_map/stj,tji->tsi/dot_general | solution.py:21
  41.2 2.2 broadcast_in_dim.19
  43.5 51.1 %scatter_fusion = f32[513,16,128]{2,1,0:T(8,128)} fusion(f32[513,16,128]{2,1,0:T(8,128)} %broadcast_in_dim.19, s32[384]{0:T(512)S(1)} %fusion.23, f32[384,16,128]{2,1,0:T(8,128)S(1)} %fusion), kind=kCustom, calls=%fused_computation.1 | custom fusion | flops 786432 | bytes 9438720 | tf_op jit(solution)/shard_map/scatter-add | solution.py:24
  94.6 4.4 %slice.21 = f32[512,16,128]{2,1,0:T(8,128)} slice(f32[513,16,128]{2,1,0:T(8,128)} %scatter_fusion), slice={[0:512], [0:16], [0:128]} | slice | bytes 8388608 | tf_op jit(solution)/shard_map/slice | solution.py:25
  99.0 0.0 reduce-scatter.2.cloned.1.call-update
  99.0 0.0 copy-start.1
  99.0 0.2 all-reduce.3.cloned.1.call-start
  99.3 18.0 %fusion.3 = f32[8,16,8,16]{3,1,2,0:T(8,128)} fusion(f32[8,16,8192]{2,1,0:T(8,128)} %param.6), kind=kOutput, calls=%fused_computation.6 | convolution fusion | flops 1610612736 | bytes 4259840 | tf_op jit(solution)/shard_map/kap,lcp->kalc/dot_general | solution.py:31
  117.3 0.0 all-reduce.3.cloned.1.call-update
  117.3 1.1 slice_bitcast_fusion
  118.4 0.1 copy.61
  118.5 70.4 %reduce-scatter.2.cloned.1.call-done = f32[64,16,128]{2,1,0:T(8,128)} async-done(((f32[512,16,128]{2,1,0:T(8,128)}), f32[64,16,128]{2,1,0:T(8,128)}) %reduce-scatter.2.cloned.1.call-update) | async-done | bytes 524304 | tf_op jit(solution)/shard_map/reduce_scatter | solution.py:25
  188.9 0.0 copy-done.1
  188.9 0.0 copy-start
  188.9 17.2 %convolution_bitcast_fusion.1 = f32[8,16,16]{1,2,0:T(8,128)S(1)} fusion(f32[8,16,8192]{2,1,0:T(8,128)} %param.6, f32[8192]{0:T(1024)S(1)} %copy-done.1, f32[64,16,128]{2,1,0:T(8,128)} %reduce-scatter.2.cloned.1.call-done), kind=kOutput, calls=%fused_computation.12 | convolution fusion | flops 201588736 | bytes 5283840 | tf_op jit(solution)/shard_map/kap,bp->kab/dot_general | solution.py:29
  206.1 0.0 copy-done
  206.1 1.0 convolution_bitcast_fusion.5
  207.1 41.0 %all-reduce = (f32[8,16,16]{1,2,0:T(8,128)S(1)}, f32[16,16]{0,1:T(8,128)S(1)}) all-reduce(f32[8,16,16]{1,2,0:T(8,128)S(1)} %convolution_bitcast_fusion.1, f32[16,16]{0,1:T(8,128)S(1)} %convolution_bitcast_fusion.5), channel_id=1, replica_groups=mesh['row'=8,'col'=4] {'row','col'}, use_global_device_ids=true, to_apply=%region_3.4 | all-reduce | flops 2304 | bytes 18432 | tf_op jit(solution)/shard_map/psum | solution.py:32
  248.1 14.4 %all-reduce.3.cloned.1.call-done = f32[8,16,8,16]{3,1,2,0:T(8,128)} async-done(((f32[8,16,8,16]{3,1,2,0:T(8,128)}), f32[8,16,8,16]{3,1,2,0:T(8,128)}) %all-reduce.3.cloned.1.call-update) | async-done | bytes 65552 | tf_op jit(solution)/shard_map/psum | solution.py:32
  262.5 1.4 convolution_bitcast_fusion.2
  263.9 0.2 convolution_bitcast_fusion.3
  264.1 0.2 fusion.11
  264.3 0.1 copy.40
  264.4 1.5 cholesky.16
  265.9 0.6 compare_reduce_fusion
  266.6 0.6 fusion.21
  267.2 1.2 custom-call.6
  268.5 0.7 copy.42
  269.1 0.7 copy.41
  269.9 6.7 %fusion.2 = f32[16,8192]{1,0:T(8,128)S(1)} fusion(f32[8,16,8192]{2,1,0:T(8,128)} %param.6, f32[8192]{0:T(1024)S(1)} %copy-done.1, f32[8,16,16]{1,2,0:T(8,128)S(1)} %get-tuple-element.12, f32[64,16,128]{2,1,0:T(8,128)S(1)} %copy-done), kind=kOutput, calls=%fused_computation.5 | convolution fusion | flops 201721856 | bytes 5808128 | tf_op jit(solution)/shard_map/kab,kap->bp/dot_general | solution.py:36
  276.6 1.4 fusion.18
  (5 shorter events, 0.1 us)
Async XLA Ops:
  8.0 22.4 %all-gather.2.cloned.1.call-start = ((), (), s32[]{:S(2)}) async-start(), calls=%async_computation.1 | async-start | bytes 1310720 | tf_op jit(solution)/shard_map/all_gather | solution.py:13
  9.8 179.0 %reduce-scatter.2.cloned.1.call-start = ((), (), s32[]{:S(2)}) async-start(), calls=%async_computation.2 | async-start | bytes 4718592 | tf_op jit(solution)/shard_map/reduce_scatter | solution.py:25
  99.0 89.8 %copy-start.1 = (f32[8192]{0:T(1024)S(1)}, f32[8192]{0:T(1024)}, u32[]{:S(2)}) copy-start(f32[8192]{0:T(1024)} %param.11) | copy-start | bytes 98308
  99.0 163.4 %all-reduce.3.cloned.1.call-start = ((), (), s32[]{:S(2)}) async-start(), calls=%async_computation.3 | async-start | bytes 1048576 | tf_op jit(solution)/shard_map/psum | solution.py:32
  188.9 17.2 %copy-start = (f32[64,16,128]{2,1,0:T(8,128)S(1)}, f32[64,16,128]{2,1,0:T(8,128)}, u32[]{:S(2)}) copy-start(f32[64,16,128]{2,1,0:T(8,128)} %reduce-scatter.2.cloned.1.call-done) | copy-start | bytes 1572868
Sparse Core Ops, SparseCore 0:
  10.9 19.4 all-gather.1
  99.1 89.6 reduce-scatter.1
Sparse Core Ops, SparseCore 1:
  117.4 145.0 all-reduce.2
where the time goes:
time: 288 us; the launch traced here: 285 us
  waiting for transfers between devices  103 us (36%)
  other arithmetic  57.3 us (20%)
  matrix products  53.1 us (18%)
  blocking collectives  41 us (14%)
  between operations  16.2 us (6%)
  local copies, waits for them, and re-layouts  15.1 us (5%)
    reduce_scatter x1, waiting for transfers between devices, local(): lax.psum_scatter(summed[:block_tiles], 'row', scatter_dimension=0, tiled=...  70.4 us
    scatter-add x1, other arithmetic, local(): jax.ops.segment_sum(products, segment_ids, num_segments=block_tiles + 1)  51.1 us
    psum x1, blocking collectives, local(): lax.psum((local_proj, local_self, local_basis), ('row', 'col'))  41 us
    dot_general x1, matrix products, local(): jnp.einsum('kap,lcp->kalc', basis_blocks, basis_blocks, precision=highest)  18 us
    all_gather x1, waiting for transfers between devices, local(): expanded = lax.all_gather(vector, 'col', axis=1, tiled=True)  17.7 us
    dot_general x1, matrix products, local(): jnp.einsum('kap,bp->kab', basis_blocks, image_rows, precision=highest)  17.2 us
    psum x1, waiting for transfers between devices, local(): lax.psum((local_proj, local_self, local_basis), ('row', 'col'))  14.4 us
    dot_general x1, matrix products, local(): jnp.einsum('stj,tji->tsi', gathered, values, preferred_element_type=jnp.f...  6.87 us
  transfers between devices with their start and end apart: 3, of which 3 were waited for; matrix products, arithmetic and copies ran while one was open for 14% of the time, Pallas kernels for 0%

commit v1 on v0

--- a/solution.py
+++ b/solution.py
@@ -10,7 +10,23 @@
     total_rows = seg_rows * lax.axis_size("row") * lax.axis_size("col")
     block_tiles = lax.axis_size("row") * seg_rows // 128
     vector = basis_blocks[-1].astype(jnp.bfloat16)
-    expanded = lax.all_gather(vector, "col", axis=1, tiled=True)
+
+    def start_series_all(view):
+        link_axis = "col"
+        n_lanes = jax.lax.axis_size(link_axis)
+        reached = [(d - 1, d) for d in range(1, n_lanes)] + [(n_lanes - 1, 0)]
+        res = view
+        by_rank = [res]
+        idx = 0
+        while idx < n_lanes - 1:
+            res = jax.lax.ppermute(res, link_axis, reached)
+            by_rank += [res]
+            idx = idx + 1
+        reply = jnp.concatenate([*reversed(by_rank)], axis=1)
+        parts_out = jnp.roll(reply, (jax.lax.axis_index(link_axis) + 1) * res.shape[1], axis=1)
+        return parts_out
+
+    expanded = start_series_all(vector)
     xblocks = expanded.reshape(rhs_width, -1, 128)
     values = tile_values[0, 0]
     row_ids = tile_rows[0, 0]

time: 288 us -> 286 us (level)
  waiting for transfers between devices: 103 us -> 100 us
    all_gather x1 -> x0, waiting for transfers between devices: 17.7 us -> none  [local(): expanded = lax.all_gather(vector, 'col', axis=1, tiled=True)]
    ppermute x0 -> x3, waiting for transfers between devices: none -> 14.8 us  [start_series_all(): res = jax.lax.ppermute(res, link_axis, reached)]
  transfers between devices with their start and end apart: 3 -> 5, of which waited for: 3 -> 5; matrix products, arithmetic and copies ran while one was open for 14% -> 14% of each run, Pallas kernels for 0% -> 0%
where the time goes in v1:
time: 286 us; the launch traced here: 284 us
  waiting for transfers between devices  100 us (35%)
  other arithmetic  57.3 us (20%)
  matrix products  53.1 us (19%)
  blocking collectives  40.9 us (14%)
  between operations  16.3 us (6%)
  local copies, waits for them, and re-layouts  15.4 us (5%)
    reduce_scatter x1, waiting for transfers between devices, local(): lax.psum_scatter(summed[:block_tiles], 'row', scatter_dimension=0, tiled=...  70.4 us
    scatter-add x1, other arithmetic, local(): jax.ops.segment_sum(products, segment_ids, num_segments=block_tiles + 1)  51.1 us
    psum x1, blocking collectives, local(): lax.psum((local_proj, local_self, local_basis), ('row', 'col'))  40.9 us
    dot_general x1, matrix products, local(): jnp.einsum('kap,lcp->kalc', basis_blocks, basis_blocks, precision=highest)  18 us
    dot_general x1, matrix products, local(): jnp.einsum('kap,bp->kab', basis_blocks, image_rows, precision=highest)  17.2 us
    psum x1, waiting for transfers between devices, local(): lax.psum((local_proj, local_self, local_basis), ('row', 'col'))  15 us
    ppermute x3, waiting for transfers between devices, start_series_all(): res = jax.lax.ppermute(res, link_axis, reached)  14.8 us
    dot_general x1, matrix products, local(): jnp.einsum('stj,tji->tsi', gathered, values, preferred_element_type=jnp.f...  6.87 us
  transfers between devices with their start and end apart: 5, of which 5 were waited for; matrix products, arithmetic and copies ran while one was open for 14% of the time, Pallas kernels for 0%

profile of v1, /device:TPU:0, one launch (start us, length us, event | category | flops | bytes accessed | tf_op | source)
XLA Modules:
  0.0 283.9 jit_solution(3104047999241812338)
XLA Ops:
  8.0 0.0 reduce-scatter.2.cloned.1.call-start
  8.0 1.1 bitcast_convert_fusion
  9.1 0.5 collective-permute-start
  9.7 6.0 %collective-permute-done = bf16[16,8192]{1,0:T(8,128)(2,1)S(1)} collective-permute-done((bf16[16,8192]{1,0:T(8,128)(2,1)S(1)}, bf16[16,8192]{1,0:T(8,128)(2,1)S(1)}, u32[]{:S(2)}, u32[]{:S(2)}) %collective-permute-start) | collective-permute-done | bytes 262176 | tf_op jit(solution)/shard_map/ppermute | solution.py:22
  15.7 0.0 collective-permute-start.1
  16.3 0.7 fusion.22
  17.0 0.7 fusion.23
  17.7 3.7 %collective-permute-done.1 = bf16[16,8192]{1,0:T(8,128)(2,1)S(1)} collective-permute-done((bf16[16,8192]{1,0:T(8,128)(2,1)S(1)}, bf16[16,8192]{1,0:T(8,128)(2,1)S(1)}, u32[]{:S(2)}, u32[]{:S(2)}) %collective-permute-start.1) | collective-permute-done | bytes 262176 | tf_op jit(solution)/shard_map/ppermute | solution.py:22
  21.5 0.0 collective-permute-start.2
  21.5 0.7 reduce.7
  22.2 5.0 %collective-permute-done.2 = bf16[16,8192]{1,0:T(8,128)(2,1)S(1)} collective-permute-done((bf16[16,8192]{1,0:T(8,128)(2,1)S(1)}, bf16[16,8192]{1,0:T(8,128)(2,1)S(1)}, u32[]{:S(2)}, u32[]{:S(2)}) %collective-permute-start.2) | collective-permute-done | bytes 262176 | tf_op jit(solution)/shard_map/ppermute | solution.py:22
  27.3 1.1 constant_dynamic-update-slice_fusion.4
  28.5 1.1 constant_dynamic-update-slice_fusion
  29.6 0.2 copy_bitcast_fusion
  29.8 2.6 gather_fusion
  32.3 6.9 %fusion = f32[384,16,128]{2,1,0:T(8,128)S(1)} fusion(bf16[1,1,384,128,128]{4,3,2,1,0:T(8,128)(2,1)} %param.7, bf16[384,16,128]{2,1,0:T(8,128)(2,1)} %gather_fusion, pred[384]{0:T(512)(128)(4,1)S(1)} %compare_and_fusion), kind=kOutput, calls=%fused_computation.2 | convolution fusion | flops 202113024 | bytes 17301888 | tf_op jit(solution)/shard_map/stj,tji->tsi/dot_general | solution.py:37
  39.2 2.2 broadcast_in_dim.19
  41.4 51.1 %scatter_fusion = f32[513,16,128]{2,1,0:T(8,128)} fusion(f32[513,16,128]{2,1,0:T(8,128)} %broadcast_in_dim.19, s32[384]{0:T(512)S(1)} %fusion.23, f32[384,16,128]{2,1,0:T(8,128)S(1)} %fusion), kind=kCustom, calls=%fused_computation.1 | custom fusion | flops 786432 | bytes 9438720 | tf_op jit(solution)/shard_map/scatter-add | solution.py:40
  92.5 4.4 %slice.21 = f32[512,16,128]{2,1,0:T(8,128)} slice(f32[513,16,128]{2,1,0:T(8,128)} %scatter_fusion), slice={[0:512], [0:16], [0:128]} | slice | bytes 8388608 | tf_op jit(solution)/shard_map/slice | solution.py:41
  97.0 0.0 reduce-scatter.2.cloned.1.call-update
  97.0 0.2 all-reduce.3.cloned.1.call-start
  97.2 18.0 %fusion.3 = f32[8,16,8,16]{3,1,2,0:T(8,128)} fusion(f32[8,16,8192]{2,1,0:T(8,128)} %param.6), kind=kOutput, calls=%fused_computation.6 | convolution fusion | flops 1610612736 | bytes 4259840 | tf_op jit(solution)/shard_map/kap,lcp->kalc/dot_general | solution.py:47
  115.2 0.0 copy-start.1
  115.2 0.0 all-reduce.3.cloned.1.call-update
  115.2 1.1 slice_bitcast_fusion
  116.3 0.1 copy.61
  116.4 70.4 %reduce-scatter.2.cloned.1.call-done = f32[64,16,128]{2,1,0:T(8,128)} async-done(((f32[512,16,128]{2,1,0:T(8,128)}), f32[64,16,128]{2,1,0:T(8,128)}) %reduce-scatter.2.cloned.1.call-update) | async-done | bytes 524304 | tf_op jit(solution)/shard_map/reduce_scatter | solution.py:41
  186.8 0.0 copy-done.1
  186.8 0.0 copy-start
  186.8 17.2 %convolution_bitcast_fusion.1 = f32[8,16,16]{1,2,0:T(8,128)S(1)} fusion(f32[8,16,8192]{2,1,0:T(8,128)} %param.6, f32[8192]{0:T(1024)S(1)} %copy-done.1, f32[64,16,128]{2,1,0:T(8,128)} %reduce-scatter.2.cloned.1.call-done), kind=kOutput, calls=%fused_computation.12 | convolution fusion | flops 201588736 | bytes 5283840 | tf_op jit(solution)/shard_map/kap,bp->kab/dot_general | solution.py:45
  204.1 0.0 copy-done
  204.1 1.0 convolution_bitcast_fusion.5
  205.1 40.9 %all-reduce = (f32[8,16,16]{1,2,0:T(8,128)S(1)}, f32[16,16]{0,1:T(8,128)S(1)}) all-reduce(f32[8,16,16]{1,2,0:T(8,128)S(1)} %convolution_bitcast_fusion.1, f32[16,16]{0,1:T(8,128)S(1)} %convolution_bitcast_fusion.5), channel_id=1, replica_groups=mesh['row'=8,'col'=4] {'row','col'}, use_global_device_ids=true, to_apply=%region_3.4 | all-reduce | flops 2304 | bytes 18432 | tf_op jit(solution)/shard_map/psum | solution.py:48
  246.0 15.0 %all-reduce.3.cloned.1.call-done = f32[8,16,8,16]{3,1,2,0:T(8,128)} async-done(((f32[8,16,8,16]{3,1,2,0:T(8,128)}), f32[8,16,8,16]{3,1,2,0:T(8,128)}) %all-reduce.3.cloned.1.call-update) | async-done | bytes 65552 | tf_op jit(solution)/shard_map/psum | solution.py:48
  260.9 1.4 convolution_bitcast_fusion.2
  262.4 0.2 convolution_bitcast_fusion.3
  262.6 0.2 fusion.11
  262.8 0.1 copy.40
  262.9 1.5 cholesky.16
  264.4 0.6 compare_reduce_fusion
  265.0 0.6 fusion.21
  265.7 1.2 custom-call.6
  266.9 0.7 copy.42
  267.6 0.7 copy.41
  268.3 6.7 %fusion.2 = f32[16,8192]{1,0:T(8,128)S(1)} fusion(f32[8,16,8192]{2,1,0:T(8,128)} %param.6, f32[8192]{0:T(1024)S(1)} %copy-done.1, f32[8,16,16]{1,2,0:T(8,128)S(1)} %get-tuple-element.12, f32[64,16,128]{2,1,0:T(8,128)S(1)} %copy-done), kind=kOutput, calls=%fused_computation.5 | convolution fusion | flops 201721856 | bytes 5808128 | tf_op jit(solution)/shard_map/kab,kap->bp/dot_general | solution.py:52
  275.1 1.4 fusion.18
  (11 shorter events, 0.2 us)
Async XLA Ops:
  8.0 178.8 %reduce-scatter.2.cloned.1.call-start = ((), (), s32[]{:S(2)}) async-start(), calls=%async_computation.1 | async-start | bytes 4718592 | tf_op jit(solution)/shard_map/reduce_scatter | solution.py:41
  9.1 6.5 %collective-permute-start = (bf16[16,8192]{1,0:T(8,128)(2,1)S(1)}, bf16[16,8192]{1,0:T(8,128)(2,1)S(1)}, u32[]{:S(2)}, u32[]{:S(2)}) collective-permute-start(bf16[16,8192]{1,0:T(8,128)(2,1)S(1)} %bitcast_convert_fusion), channel_id=1, source_target_pairs={{0,1},{1,2},{2,3},{3,0},{4,5},{5,6},{6,7},{7,4},{8,9},{9,10},{10,1... | collective-permute-start | bytes 786440 | tf_op jit(solution)/shard_map/ppermute | solution.py:22
  15.7 5.8 %collective-permute-start.1 = (bf16[16,8192]{1,0:T(8,128)(2,1)S(1)}, bf16[16,8192]{1,0:T(8,128)(2,1)S(1)}, u32[]{:S(2)}, u32[]{:S(2)}) collective-permute-start(bf16[16,8192]{1,0:T(8,128)(2,1)S(1)} %collective-permute-done), channel_id=1, source_target_pairs={{0,1},{1,2},{2,3},{3,0},{4,5},{5,6},{6,7},{7,4},{8,9},{9,10},{10,1... | collective-permute-start | bytes 786440 | tf_op jit(solution)/shard_map/ppermute | solution.py:22
  21.5 5.8 %collective-permute-start.2 = (bf16[16,8192]{1,0:T(8,128)(2,1)S(1)}, bf16[16,8192]{1,0:T(8,128)(2,1)S(1)}, u32[]{:S(2)}, u32[]{:S(2)}) collective-permute-start(bf16[16,8192]{1,0:T(8,128)(2,1)S(1)} %collective-permute-done.1), channel_id=1, source_target_pairs={{0,1},{1,2},{2,3},{3,0},{4,5},{5,6},{6,7},{7,4},{8,9},{9,10},{10,1... | collective-permute-start | bytes 786440 | tf_op jit(solution)/shard_map/ppermute | solution.py:22
  97.0 164.0 %all-reduce.3.cloned.1.call-start = ((), (), s32[]{:S(2)}) async-start(), calls=%async_computation.2 | async-start | bytes 1048576 | tf_op jit(solution)/shard_map/psum | solution.py:48
  115.2 71.6 %copy-start.1 = (f32[8192]{0:T(1024)S(1)}, f32[8192]{0:T(1024)}, u32[]{:S(2)}) copy-start(f32[8192]{0:T(1024)} %param.11) | copy-start | bytes 98308
  186.8 17.2 %copy-start = (f32[64,16,128]{2,1,0:T(8,128)S(1)}, f32[64,16,128]{2,1,0:T(8,128)}, u32[]{:S(2)}) copy-start(f32[64,16,128]{2,1,0:T(8,128)} %reduce-scatter.2.cloned.1.call-done) | copy-start | bytes 1572868
Sparse Core Ops, SparseCore 0:
  97.1 89.6 reduce-scatter.1
Sparse Core Ops, SparseCore 1:
  115.3 145.6 all-reduce.2
